TPU v7x, 32 devices: a whole 2x2x4 slice. The times are simulated.
32 devices in a mesh: mem: 4 (over y, x), tile: 8 (over z, core).
Axes of the slice: x: 2, y: 2, z: 4, core: 2. Of those that a mesh axis runs over, the one named last changes fastest.
Arguments:
- ensemble: float32 [1024, 3, 64, 256], P('mem', None, 'tile'), may hold values from -4.5 to 5
- obs_cells: int32 [8, 256], replicated, may hold values from 0 to 6143
- region_tile: int32 [8], replicated, may hold values from 0 to 7, each once
- obs_values: float32 [8, 256], replicated, may hold values from -5.6 to 5.6
- obs_error: float32 [8, 256], replicated, may hold values from 0.05 to 0.75
Outputs:
- analysis: float32 [1024, 3, 64, 256], P('mem', None, 'tile')
Inputs may be any that keep to these rules, and one draw needn't show every extreme that they name: `obs_cells`: row r lists flat indices into the values of tile region_tile[r], ordered by field, then row within the tile, then column; indices may repeat. `region_tile`: each tile holds exactly one region.
All inputs are finite; a program needn't handle non-finite values.
Results may differ from a plain program's by a relative error of at most 0.00029.
Values sent between devices are 32-bit elements; how exact they have to be, the bound alone decides.
No kernel may reach another device: no remote copies, remote signals or barrier semaphores. Data moves between devices by JAX's collectives and lax.ppermute only.
A program may use at most 128 MiB of HBM per device.

v0:
```python
import math
import jax
import jax.numpy as jnp
from jax import lax
from jax.sharding import PartitionSpec as P

ENSEMBLE_SIZE = 1024
STEPS = 4
DEGREE = 4
DEPTH = 1.0
GRAVITY = 1.0
CORIOLIS = 0.5
TIMESTEP = 0.3
DIFFUSE = 0.1
PRECISE = lax.Precision.HIGHEST


def with_halo(cells, sides, width):
    for axis, dim in sides:
        count = lax.axis_size(axis)
        head = lax.slice_in_dim(cells, 0, width, axis=dim)
        tail = lax.slice_in_dim(cells, cells.shape[dim] - width, cells.shape[dim], axis=dim)
        cells = jnp.concatenate(
            [
                lax.ppermute(tail, axis, [(i, (i + 1) % count) for i in range(count)]),
                cells,
                lax.ppermute(head, axis, [((i + 1) % count, i) for i in range(count)]),
            ],
            axis=dim,
        )
    return cells


def east_diff(quantity):
    return 0.5 * (jnp.roll(quantity, -1, axis=-1) - jnp.roll(quantity, 1, axis=-1))


def north_diff(quantity):
    return 0.5 * (quantity[:, 2:] - quantity[:, :-2])


def interior(quantity):
    return quantity[:, 1:-1]


def smoothing(quantity):
    middle = interior(quantity)
    return (
        jnp.roll(middle, -1, axis=-1)
        + jnp.roll(middle, 1, axis=-1)
        + quantity[:, 2:]
        + quantity[:, :-2]
        - 4.0 * middle
    )


def advance(padded):
    height = padded[:, 0]
    eastward = padded[:, 1]
    northward = padded[:, 2]
    height_mid = interior(height)
    east_mid = interior(eastward)
    north_mid = interior(northward)
    column = DEPTH + height
    height_rate = -(interior(east_diff(column * eastward)) + north_diff(column * northward))
    east_rate = (
        -(east_mid * interior(east_diff(eastward)) + north_mid * north_diff(eastward))
        - GRAVITY * interior(east_diff(height))
        + CORIOLIS * north_mid
    )
    north_rate = (
        -(east_mid * interior(east_diff(northward)) + north_mid * north_diff(northward))
        - GRAVITY * north_diff(height)
        - CORIOLIS * east_mid
    )
    return jnp.stack(
        [
            height_mid + TIMESTEP * height_rate + DIFFUSE * smoothing(height),
            east_mid + TIMESTEP * east_rate + DIFFUSE * smoothing(eastward),
            north_mid + TIMESTEP * north_rate + DIFFUSE * smoothing(northward),
        ],
        axis=1,
    )


def innovations(observed, target, variance, weight):
    obs_mean = jnp.mean(observed, axis=0)
    perturbed = (observed - obs_mean) * weight
    misfit = (target - obs_mean) * weight
    spread = jnp.sum(perturbed * perturbed, axis=0) / (observed.shape[0] - 1)
    return (perturbed, misfit, jnp.sum(misfit * misfit), jnp.sum(weight * (spread + variance)))


def gram_terms(perturbed, misfit, variance):
    weighted_matrix = perturbed / variance
    product = jnp.einsum("mo,no->mn", weighted_matrix, perturbed, precision=PRECISE)
    projected = jnp.dot(perturbed, misfit / variance, precision=PRECISE)
    return (product, projected)


def spectral_map(gram_scaled):
    upper_bound = 2.0 + jnp.sqrt(jnp.sum(gram_scaled * gram_scaled))
    order_count = gram_scaled.shape[0]
    shifted = 2.0 / (upper_bound - 1.0) * gram_scaled - jnp.eye(order_count, dtype=jnp.float32)
    orders = jnp.arange(DEGREE + 1, dtype=jnp.float32)
    angles = (orders + 0.5) * (math.pi / (DEGREE + 1))
    levels = 0.5 * (upper_bound + 1.0) + 0.5 * (upper_bound - 1.0) * jnp.cos(angles)
    values = lax.rsqrt(levels)
    cos_table = jnp.cos(orders[:, None] * angles[None, :])
    coeffs = 2.0 / (DEGREE + 1) * jnp.sum(cos_table * values[None, :], axis=1)
    coeffs = coeffs * jnp.where(orders == 0.0, 0.5, 1.0)
    return (shifted, coeffs)


def chebyshev(shifted, operand, coeffs):
    previous = operand
    current = jnp.dot(shifted, operand, precision=PRECISE)
    summed = coeffs[0] * previous + coeffs[1] * current
    for term_index in range(2, DEGREE + 1):
        following = 2.0 * jnp.dot(shifted, current, precision=PRECISE) - previous
        summed = summed + coeffs[term_index] * following
        previous, current = (current, following)
    return summed


def analyse(columns, product, projected, inflation):
    gram_scaled = inflation / (ENSEMBLE_SIZE - 1) * product
    shifted, coeffs = spectral_map(gram_scaled)
    centre = jnp.mean(columns, axis=0)
    spread = columns - centre
    shaped = chebyshev(shifted, spread, coeffs)
    weights = (
        inflation
        / (ENSEMBLE_SIZE - 1)
        * chebyshev(shifted, chebyshev(shifted, projected, coeffs), coeffs)
    )
    mean_shift = jnp.dot(weights, spread, precision=PRECISE)
    return centre + jnp.sqrt(inflation) * shaped + mean_shift


def on_device(ensemble, obs_cells, region_tile, obs_values, obs_error):
    layered_arrays = ensemble
    for repeat in range(STEPS):
        layered_arrays = advance(with_halo(layered_arrays, (("tile", 2),), 1))
    chosen = (region_tile == lax.axis_index("tile"))[:, None]
    obs_index = jnp.sum(jnp.where(chosen, obs_cells, 0), axis=0)
    target = jnp.sum(jnp.where(chosen, obs_values, 0.0), axis=0)
    variance = jnp.sum(jnp.where(chosen, obs_error, 0.0), axis=0)
    flat_state = layered_arrays.reshape(layered_arrays.shape[0], -1)
    columns = lax.all_to_all(flat_state, "mem", split_axis=1, concat_axis=0, tiled=True)
    selected_entries = jnp.take(flat_state, obs_index, axis=1)
    observed = lax.all_gather(selected_entries, "mem", axis=0, tiled=True)
    unit = jnp.ones(target.shape, jnp.float32)
    perturbed, misfit, misfit_sum, spread_sum = innovations(observed, target, variance, unit)
    misfit_sum, spread_sum = lax.psum((misfit_sum, spread_sum), "tile")
    product, projected = gram_terms(perturbed, misfit, variance)
    inflation = misfit_sum / spread_sum
    updated = analyse(columns, product, projected, inflation)
    restored_fields = lax.all_to_all(updated, "mem", split_axis=0, concat_axis=1, tiled=True)
    return restored_fields.reshape(ensemble.shape)


def solution(mesh):
    in_specs = (P("mem", None, "tile", None), P(), P(), P(), P())
    out_specs = P("mem", None, "tile", None)
    return jax.shard_map(
        on_device, mesh=mesh, in_specs=in_specs, out_specs=out_specs, check_vma=False
    )
```

profile of v0, /device:TPU:0, one launch (start us, length us, event | category | flops | bytes accessed | tf_op | source)
XLA Modules:
  0.0 589.1 jit_solution(11982423487698862288)
XLA Ops:
  6.5 6.6 %copy.15 = f32[256,3,8,256]{0,3,2,1:T(8,128)} copy(f32[256,3,8,256]{3,2,1,0:T(8,128)} %param.5) | data formatting | bytes 12582912 | tf_op args[0]
  15.1 4.1 collective-permute-start.1
  19.2 15.4 %collective-permute-done = f32[256,3,1,256]{0,3,2,1:T(8,128)S(1)} collective-permute-done((f32[256,3,1,256]{0,3,2,1:T(8,128)S(1)}, f32[256,3,1,256]{0,3,2,1:T(8,128)S(1)}, u32[]{:S(2)}, u32[]{:S(2)}) %collective-permute-start) | collective-permute-done | bytes 786464 | tf_op jit(solution)/shard_map/ppermute | solution.py:25
  35.1 3.2 pad_maximum_fusion
  39.9 2.7 fusion.250
  42.7 2.3 fusion.258
  45.0 2.9 fusion.260
  47.9 3.5 fusion.248
  51.4 3.5 fusion.254
  54.9 4.9 fusion.110
  59.9 3.8 fusion.130
  65.0 4.6 fusion.118
  71.8 2.4 collective-permute-start.3
  74.2 14.4 %collective-permute-done.2 = f32[256,3,1,256]{0,3,2,1:T(8,128)S(1)} collective-permute-done((f32[256,3,1,256]{0,3,2,1:T(8,128)S(1)}, f32[256,3,1,256]{0,3,2,1:T(8,128)S(1)}, u32[]{:S(2)}, u32[]{:S(2)}) %collective-permute-start.2) | collective-permute-done | bytes 786464 | tf_op jit(solution)/shard_map/ppermute | solution.py:25
  91.6 2.8 fusion.236
  94.4 2.4 fusion.234
  96.8 2.3 fusion.244
  99.1 2.4 fusion.238
  104.6 4.6 fusion.77
  109.3 4.2 fusion.97
  113.4 5.6 fusion.85
  120.9 2.4 collective-permute-start.4
  124.8 14.8 %collective-permute-done.4 = f32[256,3,1,256]{0,3,2,1:T(8,128)S(1)} collective-permute-done((f32[256,3,1,256]{0,3,2,1:T(8,128)}, f32[256,3,1,256]{0,3,2,1:T(8,128)S(1)}, u32[]{:S(2)}, u32[]{:S(2)}) %collective-permute-start.4) | collective-permute-done | bytes 786464 | tf_op jit(solution)/shard_map/ppermute | solution.py:25
  140.9 2.8 pad_maximum_fusion.2
  147.3 2.4 fusion.220
  153.7 2.8 fusion.232
  157.1 4.6 fusion.44
  161.7 3.8 fusion.64
  165.5 4.6 fusion.52
  172.4 2.1 collective-permute-start.7
  175.1 13.7 %collective-permute-done.6 = f32[256,3,1,256]{0,3,2,1:T(8,128)S(1)} collective-permute-done((f32[256,3,1,256]{0,3,2,1:T(8,128)S(1)}, f32[256,3,1,256]{0,3,2,1:T(8,128)S(1)}, u32[]{:S(2)}, u32[]{:S(2)}) %collective-permute-start.6) | collective-permute-done | bytes 786464 | tf_op jit(solution)/shard_map/ppermute | solution.py:25
  192.7 2.3 fusion.206
  195.0 2.4 fusion.216
  200.8 5.3 fusion.11
  206.1 4.0 fusion.31
  210.1 3.4 fusion.19
  213.5 3.3 pad_maximum_fusion.4
  216.8 3.8 gather_fusion
  221.5 5.3 all-to-all-start
  226.8 62.4 %all-gather.2.cloned.1.call-done = f32[1024,256]{0,1:T(8,128)} async-done(((f32[256,256]{0,1:T(8,128)}), f32[1024,256]{0,1:T(8,128)}) %all-gather.2.cloned.1.call-update) | async-done | bytes 1048592 | tf_op jit(solution)/shard_map/all_gather | solution.py:152
  293.4 17.0 %all-reduce = (f32[]{:T(128)}, f32[]{:T(128)}) all-reduce(f32[]{:T(128)} %get-tuple-element.150, f32[]{:T(128)} %add_reduce_fusion), channel_id=1, replica_groups=mesh['mem'=4,'tile'=8] {'tile'}, use_global_device_ids=true, to_apply=%region_5.6 | all-reduce | flops 2 | bytes 16 | tf_op jit(solution)/shard_map/psum | solution.py:155
  311.8 7.0 %multiply_reduce_fusion = (f32[]{:T(128)}, f32[1024,1024]{1,0:T(8,128)}) fusion(f32[]{:T(128)S(6)} %div.46, f32[1024,256]{0,1:T(8,128)S(1)} %copy-done.10, f32[256]{0:T(256)S(1)} %get-tuple-element.151, f32[256]{0:T(256)S(1)} %get-tuple-element.6), kind=kOutput, calls=%fused_computation.12 | convolution fusion | flops 3225157632 | bytes 5244936 | tf_op jit(solution)/shard_map/mo,no->mn/dot_general | solution.py:96
  321.1 6.2 %fusion.193 = f32[1,1024]{1,0:T(1,128)S(1)} fusion(f32[1,1024]{1,0:T(1,128)S(1)} %fusion.184, f32[1024,1024]{1,0:T(8,128)} %get-tuple-element.158, f32[]{:T(128)S(6)} %div.49, f32[]{:T(128)S(6)} %div.46), kind=kOutput, calls=%fused_computation.291 | convolution fusion | flops 17825792 | bytes 4202504 | tf_op jit(solution)/shard_map/dot_general | solution.py:117
  327.4 3.9 fusion.191
  331.3 3.9 fusion.201
  335.3 4.1 fusion.200
  339.4 3.1 multiply_add_fusion
  342.5 3.9 fusion.199
  346.4 3.9 fusion.189
  350.3 3.9 fusion.198
  354.3 4.3 fusion.197
  358.6 3.1 add_multiply_fusion.8
  361.7 3.1 reduce_sum.92
  364.9 6.6 %copy.18 = f32[4,256,1536]{2,1,0:T(8,128)} copy(f32[4,256,1536]{1,2,0:T(8,128)} %bitcast.30) | data formatting | bytes 12582912 | tf_op jit(solution)/shard_map/all_to_all | solution.py:150
  371.4 3.6 bitcast_subtract_fusion
  375.4 20.7 %fusion.203 = f32[1024,1536]{1,0:T(8,128)S(1)} fusion(f32[1024,1536]{1,0:T(8,128)S(1)} %bitcast_subtract_fusion, f32[1024,1024]{1,0:T(8,128)S(1)} %copy-done.1, f32[]{:T(128)S(6)} %div.49, f32[]{:T(128)S(6)} %div.46), kind=kOutput, calls=%fused_computation.319 | convolution fusion | flops 19332595712 | bytes 16777224 | tf_op jit(solution)/shard_map/dot_general | solution.py:117
  396.1 3.1 convolution_reduce_fusion
  399.2 21.6 %multiply_subtract_fusion.1 = f32[1024,1536]{1,0:T(8,128)S(1)} fusion(f32[1024,1536]{1,0:T(8,128)S(1)} %bitcast_subtract_fusion, f32[1024,1536]{1,0:T(8,128)S(1)} %fusion.203, f32[1024,1024]{1,0:T(8,128)S(1)} %copy-done.1, f32[]{:T(128)S(6)} %div.49, f32[]{:T(128)S(6)} %div.46), kind=kOutput, calls=%fused_computation.9 | convolution fusion | flops 19335741440 | bytes 23068680 | tf_op jit(solution)/shard_map/dot_general | solution.py:120
  420.8 2.7 copy-done.21
  423.5 22.3 %fusion.202 = f32[1024,1536]{1,0:T(8,128)} fusion(f32[1024,1536]{1,0:T(8,128)S(1)} %multiply_subtract_fusion.1, f32[1024,1024]{1,0:T(8,128)S(1)} %copy-done.1, f32[]{:T(128)S(6)} %div.49, f32[]{:T(128)S(6)} %div.46), kind=kOutput, calls=%fused_computation.318 | convolution fusion | flops 19332595712 | bytes 16777224 | tf_op jit(solution)/shard_map/dot_general | solution.py:120
  445.8 32.6 %add_add_fusion = f32[1024,1536]{1,0:T(8,128)} fusion(f32[1024,1536]{1,0:T(8,128)} %copy-done.21, f32[1024,1536]{1,0:T(8,128)} %copy-done.20, f32[1024,1536]{1,0:T(8,128)S(1)} %bitcast_subtract_fusion, f32[1024,1536]{1,0:T(8,128)} %fusion.202, f32[1536]{0:T(1024)S(1)} %convolution_reduce_fusion, f32[]{:T(128)} %bitcast.35, f32[]{:T(128)} %bitcast.34, ...), kind=kOutput, calls=%fused_computation.7 | convolution fusion | flops 19360907264 | bytes 35663904 | tf_op jit(solution)/shard_map/dot_general | solution.py:120
  478.4 88.7 %all_to_all.35 = f32[4,256,1536]{2,1,0:T(8,128)S(1)} all-to-all(f32[4,256,1536]{2,1,0:T(8,128)} %bitcast.135), channel_id=1, replica_groups=mesh['mem'=4,'tile'=8] {'mem'}, dimensions={0} | all-to-all | bytes 12582912 | tf_op jit(solution)/shard_map/all_to_all | solution.py:159
  567.1 6.7 %copy.19 = f32[256,4,1536]{2,1,0:T(4,128)} copy(f32[256,4,1536]{2,0,1:T(8,128)S(1)} %bitcast.134) | data formatting | bytes 12582912 | tf_op jit(solution)/shard_map/all_to_all | solution.py:159
  573.8 8.3 %reshape.53 = f32[256,3,8,256]{3,2,1,0:T(8,128)} reshape(f32[256,4,1536]{2,1,0:T(4,128)} %copy.19) | data formatting | bytes 12582912 | tf_op jit(solution)/shard_map/reshape | solution.py:160
  (129 shorter events, 43.5 us)
Async XLA Ops:
  6.5 282.7 %all-gather.2.cloned.1.call-start = ((), (), s32[]{:S(2)}) async-start(), calls=%async_computation.2 | async-start | bytes 1310720 | tf_op jit(solution)/shard_map/all_gather | solution.py:152
  14.6 20.1 %collective-permute-start = (f32[256,3,1,256]{0,3,2,1:T(8,128)S(1)}, f32[256,3,1,256]{0,3,2,1:T(8,128)S(1)}, u32[]{:S(2)}, u32[]{:S(2)}) collective-permute-start(f32[256,3,1,256]{0,3,2,1:T(8,128)S(1)} %get-tuple-element.35), channel_id=1, source_target_pairs={{0,1},{1,2},{2,3},{3,4},{4,5},{5,6},{6,7},{7,0},{8,9},{9,10},{10,1... | collective-permute-start | bytes 2359304 | tf_op jit(solution)/shard_map/ppermute | solution.py:25
  15.1 20.0 %collective-permute-start.1 = (f32[256,3,1,256]{0,3,2,1:T(8,128)S(1)}, f32[256,3,1,256]{0,3,2,1:T(8,128)S(1)}, u32[]{:S(2)}, u32[]{:S(2)}) collective-permute-start(f32[256,3,1,256]{0,3,2,1:T(8,128)S(1)} %get-tuple-element.36), channel_id=1, source_target_pairs={{1,0},{2,1},{3,2},{4,3},{5,4},{6,5},{7,6},{0,7},{9,8},{10,9},{11,1... | collective-permute-start | bytes 2359304 | tf_op jit(solution)/shard_map/ppermute | solution.py:27
  54.9 5.0 copy-start.9
  54.9 5.0 copy-start.14
  59.8 3.8 copy-start.4
  59.9 3.8 copy-start.5
  59.9 4.6 copy-start.6
  59.9 5.2 copy-start.13
  69.8 18.8 %collective-permute-start.2 = (f32[256,3,1,256]{0,3,2,1:T(8,128)S(1)}, f32[256,3,1,256]{0,3,2,1:T(8,128)S(1)}, u32[]{:S(2)}, u32[]{:S(2)}) collective-permute-start(f32[256,3,1,256]{0,3,2,1:T(8,128)S(1)} %get-tuple-element.33), channel_id=1, source_target_pairs={{0,1},{1,2},{2,3},{3,4},{4,5},{5,6},{6,7},{7,0},{8,9},{9,10},{10,1... | collective-permute-start | bytes 2359304 | tf_op jit(solution)/shard_map/ppermute | solution.py:25
  71.8 17.3 %collective-permute-start.3 = (f32[256,3,1,256]{0,3,2,1:T(8,128)S(1)}, f32[256,3,1,256]{0,3,2,1:T(8,128)S(1)}, u32[]{:S(2)}, u32[]{:S(2)}) collective-permute-start(f32[256,3,1,256]{0,3,2,1:T(8,128)S(1)} %get-tuple-element.34), channel_id=1, source_target_pairs={{1,0},{2,1},{3,2},{4,3},{5,4},{6,5},{7,6},{0,7},{9,8},{10,9},{11,1... | collective-permute-start | bytes 2359304 | tf_op jit(solution)/shard_map/ppermute | solution.py:27
  104.6 4.7 copy-start.7
  113.4 5.6 copy-start.2
  119.1 1.8 copy-start.3
  120.9 18.8 %collective-permute-start.4 = (f32[256,3,1,256]{0,3,2,1:T(8,128)}, f32[256,3,1,256]{0,3,2,1:T(8,128)S(1)}, u32[]{:S(2)}, u32[]{:S(2)}) collective-permute-start(f32[256,3,1,256]{0,3,2,1:T(8,128)} %get-tuple-element.31), channel_id=1, source_target_pairs={{0,1},{1,2},{2,3},{3,4},{4,5},{5,6},{6,7},{7,0},{8,9},{9,10},{10,1... | collective-permute-start | bytes 2359304 | tf_op jit(solution)/shard_map/ppermute | solution.py:25
  123.3 17.6 %collective-permute-start.5 = (f32[256,3,1,256]{0,3,2,1:T(8,128)}, f32[256,3,1,256]{0,3,2,1:T(8,128)}, u32[]{:S(2)}, u32[]{:S(2)}) collective-permute-start(f32[256,3,1,256]{0,3,2,1:T(8,128)} %get-tuple-element.32), channel_id=1, source_target_pairs={{1,0},{2,1},{3,2},{4,3},{5,4},{6,5},{7,6},{0,7},{9,8},{10,9},{11,1... | collective-permute-start | bytes 2359304 | tf_op jit(solution)/shard_map/ppermute | solution.py:27
  157.0 4.6 copy-start.8
  170.1 4.3 copy-start.19
  170.2 4.3 copy-start.17
  170.3 18.4 %collective-permute-start.6 = (f32[256,3,1,256]{0,3,2,1:T(8,128)S(1)}, f32[256,3,1,256]{0,3,2,1:T(8,128)S(1)}, u32[]{:S(2)}, u32[]{:S(2)}) collective-permute-start(f32[256,3,1,256]{0,3,2,1:T(8,128)S(1)} %get-tuple-element.29), channel_id=1, source_target_pairs={{0,1},{1,2},{2,3},{3,4},{4,5},{5,6},{6,7},{7,0},{8,9},{9,10},{10,1... | collective-permute-start | bytes 2359304 | tf_op jit(solution)/shard_map/ppermute | solution.py:25
  172.4 17.3 %collective-permute-start.7 = (f32[256,3,1,256]{0,3,2,1:T(8,128)S(1)}, f32[256,3,1,256]{0,3,2,1:T(8,128)S(1)}, u32[]{:S(2)}, u32[]{:S(2)}) collective-permute-start(f32[256,3,1,256]{0,3,2,1:T(8,128)S(1)} %get-tuple-element.30), channel_id=1, source_target_pairs={{1,0},{2,1},{3,2},{4,3},{5,4},{6,5},{7,6},{0,7},{9,8},{10,9},{11,1... | collective-permute-start | bytes 2359304 | tf_op jit(solution)/shard_map/ppermute | solution.py:27
  206.1 4.0 copy-start.11
  210.1 3.4 copy-start.12
  216.8 3.8 copy-start.18
  216.8 4.7 copy-start.15
  216.8 4.7 copy-start.16
  221.5 140.2 %all-to-all-start = ((f32[256,4,1536]{0,2,1:T(8,128)}), f32[256,4,1536]{0,2,1:T(8,128)}, u32[]{:S(2)}, u32[]{:S(2)}) async-start(f32[256,4,1536]{0,2,1:T(8,128)} %bitcast.133), calls=%async_computation | async-start | bytes 12582912 | tf_op jit(solution)/shard_map/all_to_all | solution.py:150
  289.2 22.6 %copy-start.10 = (f32[1024,256]{0,1:T(8,128)S(1)}, f32[1024,256]{0,1:T(8,128)}, u32[]{:S(2)}) copy-start(f32[1024,256]{0,1:T(8,128)} %all-gather.2.cloned.1.call-done) | copy-start | bytes 3145732
  321.1 6.3 %copy-start = (f32[1024,1024]{1,0:T(8,128)S(1)}, f32[1024,1024]{1,0:T(8,128)}, u32[]{:S(2)}) copy-start(f32[1024,1024]{1,0:T(8,128)} %get-tuple-element.158) | copy-start | bytes 12582916
  371.4 4.0 copy-start.1
  396.1 3.1 copy-start.20
  420.8 2.7 copy-start.21
Sparse Core Ops, SparseCore 0:
  221.5 67.6 all-gather.1
where the time goes:
time: 597 us; the launch traced here: 589 us
  matrix products  142 us (24%)
  waiting for transfers between devices  124 us (21%)
  blocking collectives  106 us (18%)
  local copies, waits for them, and re-layouts  90.5 us (15%)
  other arithmetic  87.9 us (15%)
  starting transfers between devices  22.3 us (4%)
  between operations  16.4 us (3%)
    dot_general x9, matrix products, chebyshev(): following = 2.0 * jnp.dot(shifted, current, precision=PRECISE) - previous  101 us
    all_to_all x1, blocking collectives, on_device(): lax.all_to_all(updated, 'mem', split_axis=0, concat_axis=1, tiled=True)  88.7 us
    all_gather x1, waiting for transfers between devices, on_device(): observed = lax.all_gather(selected_entries, 'mem', axis=0, tiled=True)  62.4 us
    ppermute x4, waiting for transfers between devices, with_halo(): lax.ppermute(tail, axis, [(i, (i + 1) % count) for i in range(count)])  58.3 us
    another operation x13, other arithmetic, advance(): jnp.stack([height_mid + TIMESTEP * height_rate + DIFFUSE * smoothing(heig...  56.7 us
    dot_general x3, matrix products, chebyshev(): current = jnp.dot(shifted, operand, precision=PRECISE)  30.8 us
    slice x22, local copies, waits for them, and re-layouts, smoothing(): jnp.roll(middle, 1, axis=-1)  25.4 us
    slice x30, local copies, waits for them, and re-layouts, east_diff(): jnp.roll(quantity, 1, axis=-1)  23.1 us
  transfers between devices with their start and end apart: 10, of which 9 were waited for; matrix products, arithmetic and copies ran while one was open for 9% of the time, Pallas kernels for 0%

commit v1 on v0

--- a/solution.py
+++ b/solution.py
@@ -13,6 +13,16 @@
 TIMESTEP = 0.3
 DIFFUSE = 0.1
 PRECISE = lax.Precision.HIGHEST
+
+
+def gather_by_hops(block, mesh_axis, along):
+    size = lax.axis_size(mesh_axis)
+    moving, blocks = (block, [block])
+    for _ in range(size - 1):
+        moving = lax.ppermute(moving, mesh_axis, [(i, (i + 1) % size) for i in range(size)])
+        blocks.insert(0, moving)
+    line = jnp.concatenate(blocks, axis=along)
+    return jnp.roll(line, (lax.axis_index(mesh_axis) + 1) * block.shape[along], axis=along)
 
 
 def with_halo(cells, sides, width):
@@ -149,7 +159,7 @@
     flat_state = layered_arrays.reshape(layered_arrays.shape[0], -1)
     columns = lax.all_to_all(flat_state, "mem", split_axis=1, concat_axis=0, tiled=True)
     selected_entries = jnp.take(flat_state, obs_index, axis=1)
-    observed = lax.all_gather(selected_entries, "mem", axis=0, tiled=True)
+    observed = gather_by_hops(selected_entries, "mem", 0)
     unit = jnp.ones(target.shape, jnp.float32)
     perturbed, misfit, misfit_sum, spread_sum = innovations(observed, target, variance, unit)
     misfit_sum, spread_sum = lax.psum((misfit_sum, spread_sum), "tile")

time: 597 us -> 524 us (0.88)
  waiting for transfers between devices: 124 us -> 81 us
  blocking collectives: 106 us -> 88.6 us
  between operations: 16.4 us -> 3.07 us
    all_gather x1 -> x0, waiting for transfers between devices: 62.4 us -> none  [on_device(): observed = lax.all_gather(selected_entries, 'mem', axis=0, tiled=True)]
    ppermute x0 -> x3, waiting for transfers between devices: none -> 18.1 us  [gather_by_hops(): lax.ppermute(moving, mesh_axis, [(i, (i + 1) % size) for i in range(size)])]
    all_to_all x1, blocking collectives: 88.7 us -> 74.3 us  [on_device(): lax.all_to_all(updated, 'mem', split_axis=0, concat_axis=1, tiled=True)]
  transfers between devices with their start and end apart: 10 -> 12, of which waited for: 9 -> 12; matrix products, arithmetic and copies ran while one was open for 9% -> 10% of each run, Pallas kernels for 0% -> 0%
where the time goes in v1:
time: 524 us; the launch traced here: 516 us
  matrix products  142 us (27%)
  local copies, waits for them, and re-layouts  90.6 us (17%)
  blocking collectives  88.6 us (17%)
  other arithmetic  84.3 us (16%)
  waiting for transfers between devices  81 us (15%)
  starting transfers between devices  26.4 us (5%)
    dot_general x9, matrix products, chebyshev(): following = 2.0 * jnp.dot(shifted, current, precision=PRECISE) - previous  101 us
    all_to_all x1, blocking collectives, on_device(): lax.all_to_all(updated, 'mem', split_axis=0, concat_axis=1, tiled=True)  74.3 us
    ppermute x4, waiting for transfers between devices, with_halo(): lax.ppermute(tail, axis, [(i, (i + 1) % count) for i in range(count)])  58.8 us
    another operation x13, other arithmetic, advance(): jnp.stack([height_mid + TIMESTEP * height_rate + DIFFUSE * smoothing(heig...  56.7 us
    dot_general x3, matrix products, chebyshev(): current = jnp.dot(shifted, operand, precision=PRECISE)  30.8 us
    slice x22, local copies, waits for them, and re-layouts, smoothing(): jnp.roll(middle, 1, axis=-1)  25.4 us
    slice x30, local copies, waits for them, and re-layouts, east_diff(): jnp.roll(quantity, 1, axis=-1)  23.1 us
    ppermute x3, waiting for transfers between devices, gather_by_hops(): lax.ppermute(moving, mesh_axis, [(i, (i + 1) % size) for i in range(size)])  18.1 us
  transfers between devices with their start and end apart: 12, of which 12 were waited for; matrix products, arithmetic and copies ran while one was open for 10% of the time, Pallas kernels for 0%

profile of v1, /device:TPU:0, one launch (start us, length us, event | category | flops | bytes accessed | tf_op | source)
XLA Modules:
  0.0 516.4 jit_solution(7031139568421119075)
XLA Ops:
  0.0 6.6 %copy.15 = f32[256,3,8,256]{0,3,2,1:T(8,128)} copy(f32[256,3,8,256]{3,2,1,0:T(8,128)} %param.5) | data formatting | bytes 12582912 | tf_op args[0]
  8.6 4.1 collective-permute-start.1
  12.7 15.4 %collective-permute-done = f32[256,3,1,256]{0,3,2,1:T(8,128)S(1)} collective-permute-done((f32[256,3,1,256]{0,3,2,1:T(8,128)S(1)}, f32[256,3,1,256]{0,3,2,1:T(8,128)S(1)}, u32[]{:S(2)}, u32[]{:S(2)}) %collective-permute-start) | collective-permute-done | bytes 786464 | tf_op jit(solution)/shard_map/ppermute | solution.py:35
  28.6 3.2 pad_maximum_fusion
  33.4 2.7 fusion.250
  38.4 2.9 fusion.260
  41.3 3.5 fusion.248
  44.9 3.5 fusion.254
  48.3 4.9 fusion.110
  53.3 3.8 fusion.130
  58.5 4.6 fusion.118
  65.3 2.4 collective-permute-start.3
  67.6 14.4 %collective-permute-done.2 = f32[256,3,1,256]{0,3,2,1:T(8,128)S(1)} collective-permute-done((f32[256,3,1,256]{0,3,2,1:T(8,128)S(1)}, f32[256,3,1,256]{0,3,2,1:T(8,128)S(1)}, u32[]{:S(2)}, u32[]{:S(2)}) %collective-permute-start.2) | collective-permute-done | bytes 786464 | tf_op jit(solution)/shard_map/ppermute | solution.py:35
  85.1 2.8 fusion.236
  87.9 2.4 fusion.234
  90.2 2.3 fusion.244
  92.6 2.4 fusion.238
  98.1 4.6 fusion.77
  102.7 4.2 fusion.97
  106.9 5.6 %fusion.85 = f32[256,1,8,256]{0,3,2,1:T(8,128)S(1)} fusion(f32[256,10,1]{0,2,1:T(1,128)S(1)} %get-tuple-element.110, f32[256,10,255]{0,2,1:T(8,128)S(1)} %get-tuple-element.112, f32[256,10,255]{0,2,1:T(8,128)S(1)} %get-tuple-element.111, f32[256,10,1]{0,2,1:T(1,128)S(1)} %get-tuple-element.109, f32[256,10,1]{0,2,1:T(1,128)S(1)} %get-tuple-element.106, ...), kind=kLoop, calls=%fused_computation.139 | loop fusion | flops 14680064 | bytes 25165824 | tf_op jit(solution)/shard_map/stack | solution.py:86
  114.4 2.4 collective-permute-start.4
  118.3 14.8 %collective-permute-done.4 = f32[256,3,1,256]{0,3,2,1:T(8,128)S(1)} collective-permute-done((f32[256,3,1,256]{0,3,2,1:T(8,128)}, f32[256,3,1,256]{0,3,2,1:T(8,128)S(1)}, u32[]{:S(2)}, u32[]{:S(2)}) %collective-permute-start.4) | collective-permute-done | bytes 786464 | tf_op jit(solution)/shard_map/ppermute | solution.py:35
  134.4 2.8 pad_maximum_fusion.2
  140.8 2.4 fusion.220
  147.2 2.8 fusion.232
  150.5 4.6 fusion.44
  155.1 3.8 fusion.64
  159.0 4.6 fusion.52
  168.0 14.1 %collective-permute-done.6 = f32[256,3,1,256]{0,3,2,1:T(8,128)S(1)} collective-permute-done((f32[256,3,1,256]{0,3,2,1:T(8,128)S(1)}, f32[256,3,1,256]{0,3,2,1:T(8,128)S(1)}, u32[]{:S(2)}, u32[]{:S(2)}) %collective-permute-start.6) | collective-permute-done | bytes 786464 | tf_op jit(solution)/shard_map/ppermute | solution.py:35
  186.2 2.3 fusion.206
  188.5 2.4 fusion.216
  194.2 5.3 %fusion.11 = f32[256,1,8,256]{0,3,2,1:T(8,128)} fusion(f32[256,10,1]{0,2,1:T(1,128)S(1)} %get-tuple-element.62, f32[256,10,255]{0,2,1:T(8,128)S(1)} %get-tuple-element.64, f32[256,10,255]{0,2,1:T(8,128)S(1)} %get-tuple-element.63, f32[256,10,1]{0,2,1:T(1,128)S(1)} %get-tuple-element.61, f32[256,8,1]{0,2,1:T(1,128)S(1)} %get-tuple-element.58, ...), kind=kLoop, calls=%fused_computation.45 | loop fusion | flops 13631488 | bytes 24117248 | tf_op jit(solution)/shard_map/stack | solution.py:86
  199.6 4.0 fusion.31
  203.6 3.4 fusion.19
  207.0 3.3 pad_maximum_fusion.4
  210.3 3.8 gather_fusion
  216.2 6.6 %collective-permute-done.8 = f32[256,256]{0,1:T(8,128)S(1)} collective-permute-done((f32[256,256]{0,1:T(8,128)S(1)}, f32[256,256]{0,1:T(8,128)S(1)}, u32[]{:S(2)}, u32[]{:S(2)}) %collective-permute-start.8) | collective-permute-done | bytes 262176 | tf_op jit(solution)/shard_map/ppermute | solution.py:22
  224.1 8.3 %collective-permute-done.9 = f32[256,256]{0,1:T(8,128)S(1)} collective-permute-done((f32[256,256]{0,1:T(8,128)S(1)}, f32[256,256]{0,1:T(8,128)S(1)}, u32[]{:S(2)}, u32[]{:S(2)}) %collective-permute-start.9) | collective-permute-done | bytes 262176 | tf_op jit(solution)/shard_map/ppermute | solution.py:22
  233.2 5.3 %all-to-all-start = ((f32[256,4,1536]{0,2,1:T(8,128)}), f32[256,4,1536]{0,2,1:T(8,128)}, u32[]{:S(2)}, u32[]{:S(2)}) async-start(f32[256,4,1536]{0,2,1:T(8,128)} %bitcast.137), calls=%async_computation | async-start | bytes 12582912 | tf_op jit(solution)/shard_map/all_to_all | solution.py:160
  238.5 3.3 collective-permute-done.10
  243.9 14.3 %all-reduce = (f32[]{:T(128)}, f32[]{:T(128)}) all-reduce(f32[]{:T(128)} %get-tuple-element.150, f32[]{:T(128)} %add_reduce_fusion), channel_id=1, replica_groups=mesh['mem'=4,'tile'=8] {'tile'}, use_global_device_ids=true, to_apply=%region_5.6 | all-reduce | flops 2 | bytes 16 | tf_op jit(solution)/shard_map/psum | solution.py:165
  259.5 7.0 %multiply_reduce_fusion = (f32[]{:T(128)}, f32[1024,1024]{1,0:T(8,128)}) fusion(f32[]{:T(128)S(6)} %div.46, f32[2048,256]{0,1:T(8,128)S(1)} %constant_dynamic-update-slice_fusion, s32[]{:T(128)S(6)} %select_n.54, f32[256]{0:T(256)S(1)} %get-tuple-element.151, f32[256]{0:T(256)S(1)} %get-tuple-element.6), kind=kOutput, calls=%fused_computation.12 | convolution fusion | flops 3225157632 | bytes 6296068 | tf_op jit(solution)/shard_map/mo,no->mn/dot_general | solution.py:106
  268.8 6.2 %fusion.191 = f32[1,1024]{1,0:T(1,128)S(1)} fusion(f32[1,1024]{1,0:T(1,128)S(1)} %fusion.183, f32[1024,1024]{1,0:T(8,128)} %get-tuple-element.158, f32[]{:T(128)S(6)} %div.49, f32[]{:T(128)S(6)} %div.46), kind=kOutput, calls=%fused_computation.299 | convolution fusion | flops 17825792 | bytes 4202504 | tf_op jit(solution)/shard_map/dot_general | solution.py:127
  275.1 3.9 fusion.189
  279.0 3.9 fusion.201
  283.0 4.1 fusion.200
  287.1 3.1 multiply_add_fusion
  290.2 3.9 fusion.199
  294.1 3.9 fusion.187
  298.0 3.9 fusion.198
  302.0 4.3 fusion.197
  306.3 3.1 add_multiply_fusion.8
  310.3 3.1 reduce_sum.92
  313.4 6.6 %copy.18 = f32[4,256,1536]{2,1,0:T(8,128)} copy(f32[4,256,1536]{1,2,0:T(8,128)} %bitcast.30) | data formatting | bytes 12582912 | tf_op jit(solution)/shard_map/all_to_all | solution.py:160
  320.0 3.6 bitcast_subtract_fusion
  324.0 20.7 %fusion.203 = f32[1024,1536]{1,0:T(8,128)S(1)} fusion(f32[1024,1536]{1,0:T(8,128)S(1)} %bitcast_subtract_fusion, f32[1024,1024]{1,0:T(8,128)S(1)} %copy-done.1, f32[]{:T(128)S(6)} %div.49, f32[]{:T(128)S(6)} %div.46), kind=kOutput, calls=%fused_computation.329 | convolution fusion | flops 19332595712 | bytes 16777224 | tf_op jit(solution)/shard_map/dot_general | solution.py:127
  344.7 3.1 convolution_reduce_fusion
  347.8 21.6 %multiply_subtract_fusion.1 = f32[1024,1536]{1,0:T(8,128)S(1)} fusion(f32[1024,1536]{1,0:T(8,128)S(1)} %bitcast_subtract_fusion, f32[1024,1536]{1,0:T(8,128)S(1)} %fusion.203, f32[1024,1024]{1,0:T(8,128)S(1)} %copy-done.1, f32[]{:T(128)S(6)} %div.49, f32[]{:T(128)S(6)} %div.46), kind=kOutput, calls=%fused_computation.9 | convolution fusion | flops 19335741440 | bytes 23068680 | tf_op jit(solution)/shard_map/dot_general | solution.py:130
  369.4 2.7 copy-done.21
  372.0 22.3 %fusion.202 = f32[1024,1536]{1,0:T(8,128)} fusion(f32[1024,1536]{1,0:T(8,128)S(1)} %multiply_subtract_fusion.1, f32[1024,1024]{1,0:T(8,128)S(1)} %copy-done.1, f32[]{:T(128)S(6)} %div.49, f32[]{:T(128)S(6)} %div.46), kind=kOutput, calls=%fused_computation.328 | convolution fusion | flops 19332595712 | bytes 16777224 | tf_op jit(solution)/shard_map/dot_general | solution.py:130
  394.3 32.6 %add_add_fusion = f32[1024,1536]{1,0:T(8,128)} fusion(f32[1024,1536]{1,0:T(8,128)} %copy-done.21, f32[1024,1536]{1,0:T(8,128)} %copy-done.20, f32[1024,1536]{1,0:T(8,128)S(1)} %bitcast_subtract_fusion, f32[1024,1536]{1,0:T(8,128)} %fusion.202, f32[1536]{0:T(1024)S(1)} %convolution_reduce_fusion, f32[]{:T(128)} %bitcast.35, f32[]{:T(128)} %bitcast.34, ...), kind=kOutput, calls=%fused_computation.7 | convolution fusion | flops 19360907264 | bytes 35663904 | tf_op jit(solution)/shard_map/dot_general | solution.py:130
  427.0 74.3 %all_to_all.35 = f32[4,256,1536]{2,1,0:T(8,128)S(1)} all-to-all(f32[4,256,1536]{2,1,0:T(8,128)} %bitcast.139), channel_id=1, replica_groups=mesh['mem'=4,'tile'=8] {'mem'}, dimensions={0} | all-to-all | bytes 12582912 | tf_op jit(solution)/shard_map/all_to_all | solution.py:169
  501.3 6.7 %copy.19 = f32[256,4,1536]{2,1,0:T(4,128)} copy(f32[256,4,1536]{2,0,1:T(8,128)S(1)} %bitcast.138) | data formatting | bytes 12582912 | tf_op jit(solution)/shard_map/all_to_all | solution.py:169
  507.9 8.3 %reshape.53 = f32[256,3,8,256]{3,2,1,0:T(8,128)} reshape(f32[256,4,1536]{2,1,0:T(4,128)} %copy.19) | data formatting | bytes 12582912 | tf_op jit(solution)/shard_map/reshape | solution.py:170
  (140 shorter events, 49.5 us)
Async XLA Ops:
  8.0 20.1 %collective-permute-start = (f32[256,3,1,256]{0,3,2,1:T(8,128)S(1)}, f32[256,3,1,256]{0,3,2,1:T(8,128)S(1)}, u32[]{:S(2)}, u32[]{:S(2)}) collective-permute-start(f32[256,3,1,256]{0,3,2,1:T(8,128)S(1)} %get-tuple-element.35), channel_id=1, source_target_pairs={{0,1},{1,2},{2,3},{3,4},{4,5},{5,6},{6,7},{7,0},{8,9},{9,10},{10,1... | collective-permute-start | bytes 2359304 | tf_op jit(solution)/shard_map/ppermute | solution.py:35
  8.6 20.0 %collective-permute-start.1 = (f32[256,3,1,256]{0,3,2,1:T(8,128)S(1)}, f32[256,3,1,256]{0,3,2,1:T(8,128)S(1)}, u32[]{:S(2)}, u32[]{:S(2)}) collective-permute-start(f32[256,3,1,256]{0,3,2,1:T(8,128)S(1)} %get-tuple-element.36), channel_id=1, source_target_pairs={{1,0},{2,1},{3,2},{4,3},{5,4},{6,5},{7,6},{0,7},{9,8},{10,9},{11,1... | collective-permute-start | bytes 2359304 | tf_op jit(solution)/shard_map/ppermute | solution.py:37
  48.3 5.0 copy-start.9
  48.3 5.0 copy-start.13
  53.3 3.8 copy-start.4
  53.3 3.8 copy-start.5
  53.3 4.6 copy-start.6
  53.3 5.2 copy-start.12
  63.2 18.8 %collective-permute-start.2 = (f32[256,3,1,256]{0,3,2,1:T(8,128)S(1)}, f32[256,3,1,256]{0,3,2,1:T(8,128)S(1)}, u32[]{:S(2)}, u32[]{:S(2)}) collective-permute-start(f32[256,3,1,256]{0,3,2,1:T(8,128)S(1)} %get-tuple-element.33), channel_id=1, source_target_pairs={{0,1},{1,2},{2,3},{3,4},{4,5},{5,6},{6,7},{7,0},{8,9},{9,10},{10,1... | collective-permute-start | bytes 2359304 | tf_op jit(solution)/shard_map/ppermute | solution.py:35
  65.3 17.3 %collective-permute-start.3 = (f32[256,3,1,256]{0,3,2,1:T(8,128)S(1)}, f32[256,3,1,256]{0,3,2,1:T(8,128)S(1)}, u32[]{:S(2)}, u32[]{:S(2)}) collective-permute-start(f32[256,3,1,256]{0,3,2,1:T(8,128)S(1)} %get-tuple-element.34), channel_id=1, source_target_pairs={{1,0},{2,1},{3,2},{4,3},{5,4},{6,5},{7,6},{0,7},{9,8},{10,9},{11,1... | collective-permute-start | bytes 2359304 | tf_op jit(solution)/shard_map/ppermute | solution.py:37
  98.1 4.7 copy-start.7
  106.9 5.6 %copy-start.2 = (f32[256,1,8,256]{0,3,2,1:T(8,128)}, f32[256,1,8,256]{0,3,2,1:T(8,128)S(1)}, u32[]{:S(2)}) copy-start(f32[256,1,8,256]{0,3,2,1:T(8,128)S(1)} %fusion.97) | copy-start | bytes 6291460
  112.5 1.8 copy-start.3
  114.4 18.8 %collective-permute-start.4 = (f32[256,3,1,256]{0,3,2,1:T(8,128)}, f32[256,3,1,256]{0,3,2,1:T(8,128)S(1)}, u32[]{:S(2)}, u32[]{:S(2)}) collective-permute-start(f32[256,3,1,256]{0,3,2,1:T(8,128)} %get-tuple-element.31), channel_id=1, source_target_pairs={{0,1},{1,2},{2,3},{3,4},{4,5},{5,6},{6,7},{7,0},{8,9},{9,10},{10,1... | collective-permute-start | bytes 2359304 | tf_op jit(solution)/shard_map/ppermute | solution.py:35
  116.8 17.6 %collective-permute-start.5 = (f32[256,3,1,256]{0,3,2,1:T(8,128)}, f32[256,3,1,256]{0,3,2,1:T(8,128)}, u32[]{:S(2)}, u32[]{:S(2)}) collective-permute-start(f32[256,3,1,256]{0,3,2,1:T(8,128)} %get-tuple-element.32), channel_id=1, source_target_pairs={{1,0},{2,1},{3,2},{4,3},{5,4},{6,5},{7,6},{0,7},{9,8},{10,9},{11,1... | collective-permute-start | bytes 2359304 | tf_op jit(solution)/shard_map/ppermute | solution.py:37
  150.5 4.6 copy-start.8
  163.6 4.3 copy-start.19
  163.6 4.3 copy-start.16
  163.8 18.4 %collective-permute-start.6 = (f32[256,3,1,256]{0,3,2,1:T(8,128)S(1)}, f32[256,3,1,256]{0,3,2,1:T(8,128)S(1)}, u32[]{:S(2)}, u32[]{:S(2)}) collective-permute-start(f32[256,3,1,256]{0,3,2,1:T(8,128)S(1)} %get-tuple-element.29), channel_id=1, source_target_pairs={{0,1},{1,2},{2,3},{3,4},{4,5},{5,6},{6,7},{7,0},{8,9},{9,10},{10,1... | collective-permute-start | bytes 2359304 | tf_op jit(solution)/shard_map/ppermute | solution.py:35
  165.8 17.3 %collective-permute-start.7 = (f32[256,3,1,256]{0,3,2,1:T(8,128)S(1)}, f32[256,3,1,256]{0,3,2,1:T(8,128)S(1)}, u32[]{:S(2)}, u32[]{:S(2)}) collective-permute-start(f32[256,3,1,256]{0,3,2,1:T(8,128)S(1)} %get-tuple-element.30), channel_id=1, source_target_pairs={{1,0},{2,1},{3,2},{4,3},{5,4},{6,5},{7,6},{0,7},{9,8},{10,9},{11,1... | collective-permute-start | bytes 2359304 | tf_op jit(solution)/shard_map/ppermute | solution.py:37
  167.9 15.2 %copy-start.17 = (pred[8]{0:T(512)(128)(4,1)}, pred[8]{0:T(512)(128)(4,1)S(1)}, u32[]{:S(2)}) copy-start(pred[8]{0:T(512)(128)(4,1)S(1)} %broadcast_compare_fusion) | copy-start | bytes 28
  199.6 4.0 copy-start.10
  203.6 3.4 copy-start.11
  210.2 22.9 %copy-start.14 = (f32[8,256]{1,0:T(8,128)S(1)}, f32[8,256]{1,0:T(8,128)}, u32[]{:S(2)}) copy-start(f32[8,256]{1,0:T(8,128)} %param.8) | copy-start | bytes 24580
  210.2 22.9 %copy-start.15 = (f32[8,256]{1,0:T(8,128)S(1)}, f32[8,256]{1,0:T(8,128)}, u32[]{:S(2)}) copy-start(f32[8,256]{1,0:T(8,128)} %param.9) | copy-start | bytes 24580
  210.3 22.9 %copy-start.18 = (pred[8]{0:T(512)(128)(4,1)S(1)}, pred[8]{0:T(512)(128)(4,1)}, u32[]{:S(2)}) copy-start(pred[8]{0:T(512)(128)(4,1)} %copy-done.17) | copy-start | bytes 28
  214.1 8.6 %collective-permute-start.8 = (f32[256,256]{0,1:T(8,128)S(1)}, f32[256,256]{0,1:T(8,128)S(1)}, u32[]{:S(2)}, u32[]{:S(2)}) collective-permute-start(f32[256,256]{0,1:T(8,128)S(1)} %select_bitcast_fusion), channel_id=1, source_target_pairs={{0,8},{8,16},{16,24},{24,0},{1,9},{9,17},{17,25},{25,1},{2,10},{10... | collective-permute-start | bytes 786440 | tf_op jit(solution)/shard_map/ppermute | solution.py:22
  222.7 9.7 %collective-permute-start.9 = (f32[256,256]{0,1:T(8,128)S(1)}, f32[256,256]{0,1:T(8,128)S(1)}, u32[]{:S(2)}, u32[]{:S(2)}) collective-permute-start(f32[256,256]{0,1:T(8,128)S(1)} %collective-permute-done.8), channel_id=1, source_target_pairs={{0,8},{8,16},{16,24},{24,0},{1,9},{9,17},{17,25},{25,1},{2,10},{10... | collective-permute-start | bytes 786440 | tf_op jit(solution)/shard_map/ppermute | solution.py:22
  232.4 9.4 %collective-permute-start.10 = (f32[256,256]{0,1:T(8,128)S(1)}, f32[256,256]{0,1:T(8,128)S(1)}, u32[]{:S(2)}, u32[]{:S(2)}) collective-permute-start(f32[256,256]{0,1:T(8,128)S(1)} %collective-permute-done.9), channel_id=1, source_target_pairs={{0,8},{8,16},{16,24},{24,0},{1,9},{9,17},{17,25},{25,1},{2,10},{10... | collective-permute-start | bytes 786440 | tf_op jit(solution)/shard_map/ppermute | solution.py:22
  233.2 77.0 %all-to-all-start = ((f32[256,4,1536]{0,2,1:T(8,128)}), f32[256,4,1536]{0,2,1:T(8,128)}, u32[]{:S(2)}, u32[]{:S(2)}) async-start(f32[256,4,1536]{0,2,1:T(8,128)} %bitcast.137), calls=%async_computation | async-start | bytes 12582912 | tf_op jit(solution)/shard_map/all_to_all | solution.py:160
  268.8 6.3 %copy-start = (f32[1024,1024]{1,0:T(8,128)S(1)}, f32[1024,1024]{1,0:T(8,128)}, u32[]{:S(2)}) copy-start(f32[1024,1024]{1,0:T(8,128)} %get-tuple-element.158) | copy-start | bytes 12582916
  320.0 4.0 copy-start.1
  344.7 3.1 copy-start.20
  369.3 2.7 copy-start.21
